TPU v7x, 32 devices: a whole 2x2x4 slice. The times are simulated.
32 devices in a mesh: grp: 2 (over y), res: 8 (over z, x), seq: 2 (over core).
Axes of the slice: x: 2, y: 2, z: 4, core: 2. Of those that a mesh axis runs over, the one named last changes fastest.
Arguments:
- aligned_activity: bfloat16 [512, 512, 256], P(('grp', 'seq'), 'res'), parts along dimension 0, may hold values from -6 to 6
- pair_state: bfloat16 [1024, 512, 128], P(('grp', 'res'), 'seq'), parts along dimension 0, may hold values from -6 to 6
- focus_scaling_vector: float32 [256], replicated, may hold values from 0.5 to 2
- combined_probe_matrix: bfloat16 [256, 1024], replicated, may hold values from -0.375 to 0.375
- sigmoid_offset_vector: float32 [256], replicated, may hold values from -4 to 4
- focus_final_matrix: bfloat16 [256, 256], replicated, may hold values from -0.375 to 0.375
- pair_norm_gain: float32 [128], replicated, may hold values from 0.5 to 2
- pair_bias_matrix: float32 [128, 8], replicated, may hold values from -36 to 36
- feedforward_scaling_vector: float32 [256], replicated, may hold values from 0.5 to 2
- feedforward_widen_matrix: bfloat16 [256, 1024], replicated, may hold values from -0.375 to 0.375
- feedforward_shrink_matrix: bfloat16 [1024, 256], replicated, may hold values from -0.1875 to 0.1875
- tensor_scaling_vector: float32 [256], replicated, may hold values from 0.5 to 2
- twin_operand_matrix: bfloat16 [256, 64], replicated, may hold values from -0.375 to 0.375
- tensor_final_matrix: bfloat16 [1024, 128], replicated, may hold values from -3 to 3
Outputs:
- alignment_output: bfloat16 [512, 512, 256], P(('grp', 'seq'), 'res'), parts along dimension 0
- pair_output: bfloat16 [1024, 512, 128], P(('grp', 'res'), 'seq'), parts along dimension 0
There are 2 independent parts, one for each index of `grp`. A program takes and returns all parts, laid end to end along the dimension named above; an argument that names none is the same for every part. Nothing has to cross between parts.
All inputs are finite; a program needn't handle non-finite values.
Results may differ from a plain program's by a relative error of at most 0.0095.
The roundings to bfloat16 on the way count: a program that leaves them out, or rounds other values in their place, can miss the bound.
Values may be sent and summed in bfloat16 or wider, within the bound.
A program may use at most 256 MiB of HBM per device.

v0:
```python
import math

import jax
import jax.numpy as jnp
from jax import lax
from jax.sharding import PartitionSpec as P


def layer_normalize(inputs, scale_gain):
    sample_expectation = jnp.mean(inputs, axis=-1, keepdims=True)
    centered = inputs - sample_expectation
    variance = jnp.mean(centered * centered, axis=-1, keepdims=True)
    return centered * lax.rsqrt(variance + 1e-05) * scale_gain


def attend_rows(probe_entries, lookup_entries, content_entries, bias_piece, first_row):
    row_count = bias_piece.shape[1]
    block_rows = math.gcd(row_count, 64)
    seq_count = probe_entries.shape[0]

    def one_block(block_index):
        offset = block_index * block_rows
        query_block = lax.dynamic_slice_in_dim(probe_entries, first_row + offset, block_rows, 1)
        bias_block = lax.dynamic_slice_in_dim(bias_piece, offset, block_rows, 1)
        scores = jnp.einsum(
            "snhd,sjhd->shnj", query_block, lookup_entries, preferred_element_type=jnp.float32
        )
        scores = scores + bias_block.astype(jnp.float32)[None]
        top_score = jnp.max(scores, axis=-1, keepdims=True)
        exponent = jnp.exp(scores - top_score)
        denominator = jnp.sum(exponent, axis=-1, keepdims=True)
        softmax_shares = (exponent / denominator).astype(jnp.bfloat16)
        mixed_entries = jnp.einsum(
            "shnj,sjhd->snhd", softmax_shares, content_entries, preferred_element_type=jnp.float32
        )
        return mixed_entries.reshape(seq_count, block_rows, -1)

    blocks = lax.map(one_block, jnp.arange(row_count // block_rows, dtype=jnp.int32))
    return jnp.moveaxis(blocks, 0, 1).reshape(seq_count, row_count, -1)


def project_mean(partial_value, seq_total, row_count, col_count, factor_width, tensor_final_matrix):
    pair_width = tensor_final_matrix.shape[1]
    sample_expectation = (
        (partial_value / seq_total)
        .astype(jnp.bfloat16)
        .reshape(row_count, factor_width, col_count, factor_width)
    )
    return jnp.einsum(
        "icje,cez->ijz",
        sample_expectation,
        tensor_final_matrix.reshape(factor_width, factor_width, pair_width),
        preferred_element_type=jnp.float32,
    )


def on_device(
    aligned_activity,
    pair_state,
    focus_scaling_vector,
    combined_probe_matrix,
    sigmoid_offset_vector,
    focus_final_matrix,
    pair_norm_gain,
    pair_bias_matrix,
    feedforward_scaling_vector,
    feedforward_widen_matrix,
    feedforward_shrink_matrix,
    tensor_scaling_vector,
    twin_operand_matrix,
    tensor_final_matrix,
):
    alignment_width = aligned_activity.shape[2]
    count_of_heads = pair_bias_matrix.shape[1]
    subspace_depth = alignment_width // count_of_heads
    factor_width = twin_operand_matrix.shape[1] // 2
    row_block = pair_state.shape[0]
    col_block = pair_state.shape[1]
    pair_norm = layer_normalize(pair_state.astype(jnp.float32), pair_norm_gain)
    bias_tile = jnp.einsum(
        "ijc,ch->hij", pair_norm, pair_bias_matrix, precision=lax.Precision.HIGHEST
    ).astype(jnp.bfloat16)
    bias_cols = lax.all_gather(bias_tile, "seq", axis=2, tiled=True)
    input_rows = lax.all_to_all(aligned_activity, "res", split_axis=0, concat_axis=1, tiled=True)
    seq_count = input_rows.shape[0]
    length = input_rows.shape[1]
    residual_state = input_rows.astype(jnp.float32)
    normalized_rows = layer_normalize(residual_state, focus_scaling_vector).astype(jnp.bfloat16)
    mapped_entries = jnp.dot(
        normalized_rows, combined_probe_matrix, preferred_element_type=jnp.float32
    )
    probe_entries = (
        (mapped_entries[..., :alignment_width] * subspace_depth ** (-0.5))
        .astype(jnp.bfloat16)
        .reshape(seq_count, length, count_of_heads, subspace_depth)
    )
    lookup_entries = (
        mapped_entries[..., alignment_width : 2 * alignment_width]
        .astype(jnp.bfloat16)
        .reshape(seq_count, length, count_of_heads, subspace_depth)
    )
    content_entries = (
        mapped_entries[..., 2 * alignment_width : 3 * alignment_width]
        .astype(jnp.bfloat16)
        .reshape(seq_count, length, count_of_heads, subspace_depth)
    )
    sigmoid_filter = jax.nn.sigmoid(
        mapped_entries[..., 3 * alignment_width :] + sigmoid_offset_vector
    )
    bias_all = lax.all_gather(bias_cols, "res", axis=1, tiled=True)
    mixed_entries = attend_rows(probe_entries, lookup_entries, content_entries, bias_all, 0)
    gated_rows = (mixed_entries * sigmoid_filter).astype(jnp.bfloat16)
    residual_state = residual_state + jnp.dot(
        gated_rows, focus_final_matrix, preferred_element_type=jnp.float32
    )
    normalized_rows = layer_normalize(residual_state, feedforward_scaling_vector).astype(
        jnp.bfloat16
    )
    hidden = jnp.maximum(
        jnp.dot(normalized_rows, feedforward_widen_matrix, preferred_element_type=jnp.float32), 0.0
    ).astype(jnp.bfloat16)
    residual_state = residual_state + jnp.dot(
        hidden, feedforward_shrink_matrix, preferred_element_type=jnp.float32
    )
    updated_state = residual_state.astype(jnp.bfloat16)
    contract = (((0,), (0,)), ((), ()))
    normalized_rows = layer_normalize(
        updated_state.astype(jnp.float32), tensor_scaling_vector
    ).astype(jnp.bfloat16)
    left_right_factors = jnp.dot(
        normalized_rows, twin_operand_matrix, preferred_element_type=jnp.float32
    ).astype(jnp.bfloat16)
    left_flat = left_right_factors[..., :factor_width].reshape(seq_count, -1)
    right_flat = left_right_factors[..., factor_width:].reshape(seq_count, -1)
    alignment_output, left_cols = (
        lax.all_to_all(updated_state, "res", split_axis=1, concat_axis=0, tiled=True),
        lax.all_to_all(left_flat, "res", split_axis=1, concat_axis=0, tiled=True),
    )
    left_all = lax.all_gather(left_cols, "seq", axis=0, tiled=True)
    right_split = lax.all_to_all(right_flat, "seq", split_axis=1, concat_axis=0, tiled=True)
    seq_axis = lax.axis_size("seq")
    res_axis = lax.axis_size("res")
    left_order = (
        left_all.reshape(seq_axis, res_axis, seq_count, -1)
        .transpose(1, 0, 2, 3)
        .reshape(left_all.shape[0], -1)
    )
    partial_value = lax.dot_general(
        left_order,
        lax.all_gather(right_split, "res", axis=0, tiled=True),
        contract,
        preferred_element_type=jnp.float32,
    )
    update = project_mean(
        partial_value, left_all.shape[0], row_block, col_block, factor_width, tensor_final_matrix
    )
    pair_output = (pair_state.astype(jnp.float32) + update).astype(jnp.bfloat16)
    return (alignment_output, pair_output)


def solution(mesh):
    return jax.shard_map(
        on_device,
        mesh=mesh,
        in_specs=(
            P(("grp", "seq"), "res", None),
            P(("grp", "res"), "seq", None),
            P(),
            P(),
            P(),
            P(),
            P(),
            P(),
            P(),
            P(),
            P(),
            P(),
            P(),
            P(),
        ),
        out_specs=(P(("grp", "seq"), "res", None), P(("grp", "res"), "seq", None)),
        check_vma=False,
    )
```

profile of v0, /device:TPU:0, one launch (start us, length us, event | category | flops | bytes accessed | tf_op | source)
XLA Modules:
  0.0 847.2 jit_solution(1262943649141944353)
XLA Ops:
  7.2 7.4 all-to-all-start
  14.7 3.5 convert_reduce_fusion
  18.2 6.0 fusion.27
  24.3 12.9 %fusion.67 = bf16[8,64,256]{2,0,1:T(8,128)(2,1)S(1)} fusion(bf16[64,256,128]{2,1,0:T(8,128)(2,1)S(1)} %copy-done.4, f32[128]{0:T(128)S(1)} %copy-done.15, f32[64,256]{1,0:T(8,128)S(1)} %add_rsqrt_fusion, f32[64,256]{1,0:T(8,128)S(1)} %broadcast_multiply_fusion, f32[128,8]{0,1:T(8,128)S(1)} %copy-done.12), kind=kOutput, calls=%fused_computation.70 | convolution fusion | flops 209846272 | bytes 4592128 | tf_op jit(solution)/shard_map/ijc,ch->hij/dot_general | solution.py:80
  37.2 2.3 all_gather.12
  39.6 107.1 %all-to-all-done = bf16[128,64,256]{2,1,0:T(8,128)(2,1)} async-done(((bf16[128,64,256]{2,1,0:T(8,128)(2,1)}), bf16[128,64,256]{2,1,0:T(8,128)(2,1)}, u32[]{:S(2)}, u32[]{:S(2)}) %all-to-all-start) | async-done | bytes 4194336 | tf_op jit(solution)/shard_map/all_to_all | solution.py:84
  146.7 3.4 fusion.43
  150.2 4.5 multiply_reduce_fusion.1
  154.8 3.3 convert_bitcast_fusion
  158.1 3.9 copy.83
  162.0 9.3 %copy.92 = f32[16,512,256]{1,2,0:T(8,128)} copy(f32[16,512,256]{2,1,0:T(8,128)} %bitcast.88) | data formatting | bytes 16777216 | tf_op jit(solution)/shard_map/convert_element_type | solution.py:87
  171.3 20.1 %fusion.85 = (bf16[16,512,1024]{2,1,0:T(8,128)(2,1)}, f32[16,512,1024]{2,1,0:T(8,128)}) fusion(bf16[256,1024]{1,0:T(8,128)(2,1)S(1)} %copy-done, f32[16,512,256]{2,1,0:T(8,128)} %bitcast.89, f32[256]{0:T(256)S(1)} %copy-done.6, f32[16,512]{1,0:T(8,128)S(1)} %rsqrt.36, f32[16,512]{1,0:T(8,128)S(1)} %div.44), kind=kOutput, calls=%fused_computation.89 | convolution fusion | flops 4311744512 | bytes 59311104 | tf_op jit(solution)/shard_map/dot_general | solution.py:89
  191.3 5.9 fusion.83
  197.3 6.4 copy.88
  203.7 6.4 copy.87
  210.0 6.4 fusion.40
  216.4 6.4 copy.86
  222.8 186.2 %while.10 = (s32[]{:T(128)}, f32[8,16,64,256]{2,3,1,0:T(8,128)}, s32[8]{0:T(128)S(1)}, bf16[16,512,8,32]{1,3,2,0:T(8,128)(2,1)}, bf16[16,512,8,32]{1,3,2,0:T(8,1...) while((s32[]{:T(128)}, f32[8,16,64,256]{2,3,1,0:T(8,128)}, ...), condition=%wide.region_7.8_spmd, body=%wide.region_4.7_spmd.sunk | while | flops 558105088 | bytes 50921660 | solution.py:38
  225.4 11.0 %fusion.105 = (f32[16,8,64]{2,1,0:T(8,128)S(1)}, f32[16,8,64,512]{3,2,1,0:T(8,128)}) fusion(f32[8,64,512]{2,1,0:T(8,128)S(1)} %copy_convert_fusion.2, bf16[16,512,8,32]{1,3,2,0:T(8,128)(2,1)} %get-tuple-element.174, bf16[16,512,8,32]{1,3,2,0:T(8,128)(2,1)} %get-tuple-element.173, s32[]{:T(128)S(6)} %select_n.5), kind=kOutput, calls=%fused_computation.86.clone.1 | convolution fusion | flops 281018880 | bytes 23101444 | tf_op jit(solution)/shard_map/while/body/eval_jaxpr/sub | solution.py:30
  236.4 8.2 fusion.106
  244.6 1.5 constant_dynamic-update-slice_fusion.2
  248.7 11.0 %fusion.105 = (f32[16,8,64]{2,1,0:T(8,128)S(1)}, f32[16,8,64,512]{3,2,1,0:T(8,128)}) fusion(f32[8,64,512]{2,1,0:T(8,128)S(1)} %copy_convert_fusion.2, bf16[16,512,8,32]{1,3,2,0:T(8,128)(2,1)} %get-tuple-element.174, bf16[16,512,8,32]{1,3,2,0:T(8,128)(2,1)} %get-tuple-element.173, s32[]{:T(128)S(6)} %select_n.5), kind=kOutput, calls=%fused_computation.86.clone.1 | convolution fusion | flops 281018880 | bytes 23101444 | tf_op jit(solution)/shard_map/while/body/eval_jaxpr/sub | solution.py:30
  259.7 8.2 fusion.106
  267.9 1.5 constant_dynamic-update-slice_fusion.2
  272.0 11.0 %fusion.105 = (f32[16,8,64]{2,1,0:T(8,128)S(1)}, f32[16,8,64,512]{3,2,1,0:T(8,128)}) fusion(f32[8,64,512]{2,1,0:T(8,128)S(1)} %copy_convert_fusion.2, bf16[16,512,8,32]{1,3,2,0:T(8,128)(2,1)} %get-tuple-element.174, bf16[16,512,8,32]{1,3,2,0:T(8,128)(2,1)} %get-tuple-element.173, s32[]{:T(128)S(6)} %select_n.5), kind=kOutput, calls=%fused_computation.86.clone.1 | convolution fusion | flops 281018880 | bytes 23101444 | tf_op jit(solution)/shard_map/while/body/eval_jaxpr/sub | solution.py:30
  283.0 8.2 fusion.106
  291.2 1.5 constant_dynamic-update-slice_fusion.2
  295.2 11.0 %fusion.105 = (f32[16,8,64]{2,1,0:T(8,128)S(1)}, f32[16,8,64,512]{3,2,1,0:T(8,128)}) fusion(f32[8,64,512]{2,1,0:T(8,128)S(1)} %copy_convert_fusion.2, bf16[16,512,8,32]{1,3,2,0:T(8,128)(2,1)} %get-tuple-element.174, bf16[16,512,8,32]{1,3,2,0:T(8,128)(2,1)} %get-tuple-element.173, s32[]{:T(128)S(6)} %select_n.5), kind=kOutput, calls=%fused_computation.86.clone.1 | convolution fusion | flops 281018880 | bytes 23101444 | tf_op jit(solution)/shard_map/while/body/eval_jaxpr/sub | solution.py:30
  306.3 8.2 fusion.106
  314.5 1.5 constant_dynamic-update-slice_fusion.2
  318.5 11.0 %fusion.105 = (f32[16,8,64]{2,1,0:T(8,128)S(1)}, f32[16,8,64,512]{3,2,1,0:T(8,128)}) fusion(f32[8,64,512]{2,1,0:T(8,128)S(1)} %copy_convert_fusion.2, bf16[16,512,8,32]{1,3,2,0:T(8,128)(2,1)} %get-tuple-element.174, bf16[16,512,8,32]{1,3,2,0:T(8,128)(2,1)} %get-tuple-element.173, s32[]{:T(128)S(6)} %select_n.5), kind=kOutput, calls=%fused_computation.86.clone.1 | convolution fusion | flops 281018880 | bytes 23101444 | tf_op jit(solution)/shard_map/while/body/eval_jaxpr/sub | solution.py:30
  329.5 8.2 fusion.106
  337.8 1.5 constant_dynamic-update-slice_fusion.2
  341.8 11.0 %fusion.105 = (f32[16,8,64]{2,1,0:T(8,128)S(1)}, f32[16,8,64,512]{3,2,1,0:T(8,128)}) fusion(f32[8,64,512]{2,1,0:T(8,128)S(1)} %copy_convert_fusion.2, bf16[16,512,8,32]{1,3,2,0:T(8,128)(2,1)} %get-tuple-element.174, bf16[16,512,8,32]{1,3,2,0:T(8,128)(2,1)} %get-tuple-element.173, s32[]{:T(128)S(6)} %select_n.5), kind=kOutput, calls=%fused_computation.86.clone.1 | convolution fusion | flops 281018880 | bytes 23101444 | tf_op jit(solution)/shard_map/while/body/eval_jaxpr/sub | solution.py:30
  352.8 8.2 fusion.106
  361.1 1.5 constant_dynamic-update-slice_fusion.2
  365.1 11.0 %fusion.105 = (f32[16,8,64]{2,1,0:T(8,128)S(1)}, f32[16,8,64,512]{3,2,1,0:T(8,128)}) fusion(f32[8,64,512]{2,1,0:T(8,128)S(1)} %copy_convert_fusion.2, bf16[16,512,8,32]{1,3,2,0:T(8,128)(2,1)} %get-tuple-element.174, bf16[16,512,8,32]{1,3,2,0:T(8,128)(2,1)} %get-tuple-element.173, s32[]{:T(128)S(6)} %select_n.5), kind=kOutput, calls=%fused_computation.86.clone.1 | convolution fusion | flops 281018880 | bytes 23101444 | tf_op jit(solution)/shard_map/while/body/eval_jaxpr/sub | solution.py:30
  376.1 8.2 fusion.106
  384.3 1.5 constant_dynamic-update-slice_fusion.2
  388.4 11.0 %fusion.105 = (f32[16,8,64]{2,1,0:T(8,128)S(1)}, f32[16,8,64,512]{3,2,1,0:T(8,128)}) fusion(f32[8,64,512]{2,1,0:T(8,128)S(1)} %copy_convert_fusion.2, bf16[16,512,8,32]{1,3,2,0:T(8,128)(2,1)} %get-tuple-element.174, bf16[16,512,8,32]{1,3,2,0:T(8,128)(2,1)} %get-tuple-element.173, s32[]{:T(128)S(6)} %select_n.5), kind=kOutput, calls=%fused_computation.86.clone.1 | convolution fusion | flops 281018880 | bytes 23101444 | tf_op jit(solution)/shard_map/while/body/eval_jaxpr/sub | solution.py:30
  399.4 8.2 fusion.106
  407.6 1.5 constant_dynamic-update-slice_fusion.2
  409.1 12.9 %copy.90 = f32[16,8,64,256]{3,2,1,0:T(8,128)} copy(f32[16,8,64,256]{2,3,0,1:T(8,128)} %bitcast.92) | data formatting | bytes 16777216 | tf_op jit(solution)/shard_map/transpose | solution.py:39
  422.0 7.1 fusion.41
  429.1 1.1 copy-done.2
  430.2 1.3 fusion.86
  431.6 3.2 copy-done.3
  434.8 1.2 multiply_reduce_fusion
  436.0 14.6 %convert_reduce_fusion.1 = (f32[16,512]{1,0:T(8,128)S(1)}, bf16[16,512,256]{1,2,0:T(8,128)(2,1)}) fusion(f32[16,512,256]{1,2,0:T(8,128)} %copy-done.3, bf16[1024,256]{1,0:T(8,128)(2,1)S(1)} %copy-done.8, f32[256]{0:T(256)S(1)} %copy-done.13, f32[16,512]{1,0:T(8,128)S(1)} %add_rsqrt_fusion.3, f32[16,512]{1,0:T(8,128)S(1)} %broadcast_multiply_fusion.3, ...), kind=kOutput, calls=%fused_computation.25 | convolution fusion | flops 8623480832 | bytes 13730816 | tf_op jit(solution)/shard_map/dot_general | solution.py:122
  450.7 3.3 fusion.31
  454.1 3.7 fusion.61
  457.9 1.3 copy.99
  459.2 2.3 all_to_all.53
  461.7 18.1 %all_to_all.65 = bf16[16,8,2048]{2,0,1:T(8,128)(2,1)} all-to-all(bf16[16,8,2048]{2,0,1:T(8,128)(2,1)S(1)} %copy.100), channel_id=1, replica_groups=mesh['grp'=2,'res'=8,'seq'=2] {'res'}, dimensions={1} | all-to-all | bytes 1048576 | tf_op jit(solution)/shard_map/all_to_all | solution.py:137
  479.9 7.9 copy.95
  488.8 2.0 all_to_all.57
  491.1 4.9 all_to_all.66
  496.0 4.6 all-to-all-start.1
  501.3 1.3 copy.101
  502.6 142.5 %all-to-all-done.1 = bf16[16,512,256]{2,0,1:T(8,128)(2,1)} async-done(((bf16[16,512,256]{2,0,1:T(8,128)(2,1)}), bf16[16,512,256]{2,0,1:T(8,128)(2,1)}, u32[]{:S(2)}, u32[]{:S(2)}) %all-to-all-start.1) | async-done | bytes 4194336 | tf_op jit(solution)/shard_map/all_to_all | solution.py:136
  645.1 5.8 copy.97
  650.9 16.2 %multiply_convert_fusion = bf16[2048,8192]{1,0:T(8,128)(2,1)} fusion(bf16[256,2048]{1,0:T(8,128)(2,1)S(1)} %bitcast.98, bf16[256,8192]{1,0:T(8,128)(2,1)} %all-gather.8.cloned.1.call-done), kind=kOutput, calls=%fused_computation.16 | convolution fusion | flops 8623489024 | bytes 38797312 | tf_op jit(solution)/shard_map/dot_general | solution.py:148
  667.1 126.6 %reshape.127 = bf16[64,32,256,32]{3,2,1,0:T(8,128)(2,1)} reshape(bf16[2048,8192]{1,0:T(8,128)(2,1)} %multiply_convert_fusion) | data formatting | bytes 67108864 | tf_op jit(solution)/shard_map/reshape | solution.py:47
  793.6 46.8 %fusion.34 = bf16[64,256,128]{2,1,0:T(8,128)(2,1)} fusion(bf16[64,256,128]{2,1,0:T(8,128)(2,1)} %param.17, bf16[64,32,256,32]{3,2,1,0:T(8,128)(2,1)} %reshape.127, bf16[32,32,128,1]{2,1,0,3:T(8,128)(2,1)S(1)} %bitcast.99), kind=kOutput, calls=%fused_computation.36 | convolution fusion | flops 4301258752 | bytes 42205184 | tf_op jit(solution)/shard_map/icje,cez->ijz/dot_general | solution.py:49
  (81 shorter events, 17.7 us)
Async XLA Ops:
  7.2 164.1 %copy-start = (bf16[256,1024]{1,0:T(8,128)(2,1)S(1)}, bf16[256,1024]{1,0:T(8,128)(2,1)}, u32[]{:S(2)}) copy-start(bf16[256,1024]{1,0:T(8,128)(2,1)} %param.19) | copy-start | bytes 1572868
  7.2 17.1 %copy-start.12 = (f32[128,8]{0,1:T(8,128)S(1)}, f32[128,8]{0,1:T(8,128)}, u32[]{:S(2)}) copy-start(f32[128,8]{0,1:T(8,128)} %param.23) | copy-start | bytes 12292
  7.2 17.1 %copy-start.15 = (f32[128]{0:T(128)S(1)}, f32[128]{0:T(128)}, u32[]{:S(2)}) copy-start(f32[128]{0:T(128)} %param.22) | copy-start | bytes 1540
  7.2 139.5 %all-to-all-start = ((bf16[128,64,256]{2,1,0:T(8,128)(2,1)}), bf16[128,64,256]{2,1,0:T(8,128)(2,1)}, u32[]{:S(2)}, u32[]{:S(2)}) async-start(bf16[128,64,256]{2,1,0:T(8,128)(2,1)} %param.16), calls=%async_computation | async-start | bytes 8388608 | tf_op jit(solution)/shard_map/all_to_all | solution.py:84
  14.6 208.2 %all-gather.4.cloned.1.call-start = ((), (), s32[]{:S(2)}) async-start(), calls=%async_computation.4 | async-start | bytes 4718592 | tf_op jit(solution)/shard_map/all_gather | solution.py:110
  14.7 9.6 %copy-start.4 = (bf16[64,256,128]{2,1,0:T(8,128)(2,1)S(1)}, bf16[64,256,128]{2,1,0:T(8,128)(2,1)}, u32[]{:S(2)}) copy-start(bf16[64,256,128]{2,1,0:T(8,128)(2,1)} %param.17) | copy-start | bytes 12582916
  39.5 461.8 %all-gather.6.cloned.1.call-start = ((), (), s32[]{:S(2)}) async-start(), calls=%async_computation.5 | async-start | bytes 1572864 | tf_op jit(solution)/shard_map/all_gather | solution.py:139
  162.0 9.3 %copy-start.6 = (f32[256]{0:T(256)S(1)}, f32[256]{0:T(256)}, u32[]{:S(2)}) copy-start(f32[256]{0:T(256)} %param.18) | copy-start | bytes 3076
  409.1 12.9 %copy-start.7 = (f32[256]{0:T(256)S(1)}, f32[256]{0:T(256)}, u32[]{:S(2)}) copy-start(f32[256]{0:T(256)} %param.20) | copy-start | bytes 3076
  422.0 8.3 copy-start.2
  422.0 8.3 copy-start.5
  431.6 3.2 copy-start.3
  431.6 4.4 copy-start.8
  431.6 4.4 copy-start.9
  431.6 4.4 copy-start.13
  436.0 18.0 %copy-start.11 = (bf16[256,64]{0,1:T(8,128)(2,1)S(1)}, bf16[256,64]{0,1:T(8,128)(2,1)}, u32[]{:S(2)}) copy-start(bf16[256,64]{0,1:T(8,128)(2,1)} %param.28) | copy-start | bytes 98308
  436.0 18.0 %copy-start.14 = (f32[256]{0:T(256)S(1)}, f32[256]{0:T(256)}, u32[]{:S(2)}) copy-start(f32[256]{0:T(256)} %param.27) | copy-start | bytes 3076
  496.0 149.1 %all-to-all-start.1 = ((bf16[16,512,256]{2,0,1:T(8,128)(2,1)}), bf16[16,512,256]{2,0,1:T(8,128)(2,1)}, u32[]{:S(2)}, u32[]{:S(2)}) async-start(bf16[16,512,256]{2,0,1:T(8,128)(2,1)} %copy.95), calls=%async_computation.1 | async-start | bytes 8388608 | tf_op jit(solution)/shard_map/all_to_all | solution.py:136
  500.5 150.4 %all-gather.8.cloned.1.call-start = ((), (), s32[]{:S(2)}) async-start(), calls=%async_computation.6 | async-start | bytes 4718592 | tf_op jit(solution)/shard_map/all_gather | solution.py:150
  667.1 126.6 %copy-start.10 = (bf16[1024,128]{1,0:T(8,128)(2,1)S(1)}, bf16[1024,128]{1,0:T(8,128)(2,1)}, u32[]{:S(2)}) copy-start(bf16[1024,128]{1,0:T(8,128)(2,1)} %param.29) | copy-start | bytes 786436
  793.6 46.8 %copy-start.1 = (bf16[256,1024]{1,0:T(8,128)(2,1)S(1)}, bf16[256,1024]{1,0:T(8,128)(2,1)}, u32[]{:S(2)}) copy-start(bf16[256,1024]{1,0:T(8,128)(2,1)} %param.19) | copy-start | bytes 1572868
Sparse Core Ops, SparseCore 0:
  39.6 119.3 all-gather.3
  480.0 7.4 all-gather.5
  503.5 137.3 all-gather.7
where the time goes:
time: 856 us; the launch traced here: 847 us
  matrix products  270 us (32%)
  waiting for transfers between devices  250 us (29%)
  local copies, waits for them, and re-layouts  230 us (27%)
  other arithmetic  40.2 us (5%)
  blocking collectives  25.3 us (3%)
  between operations  14.4 us (2%)
  starting transfers between devices  12.1 us (1%)
    all_to_all x1, waiting for transfers between devices, on_device(): lax.all_to_all(updated_state, 'res', split_axis=1, concat_axis=0, tiled=T...  142 us
    reshape x1, local copies, waits for them, and re-layouts, project_mean(): sample_expectation = (partial_value / seq_total).astype(jnp.bfloat16).res...  127 us
    all_to_all x1, waiting for transfers between devices, on_device(): lax.all_to_all(aligned_activity, 'res', split_axis=0, concat_axis=1, tile...  107 us
    sub x8, matrix products, one_block(): exponent = jnp.exp(scores - top_score)  88.2 us
    dot_general x8, matrix products, one_block(): jnp.einsum('shnj,sjhd->snhd', softmax_shares, content_entries, preferred_...  65.9 us
    dot_general x1, matrix products, project_mean(): jnp.einsum('icje,cez->ijz', sample_expectation, tensor_final_matrix.resha...  46.8 us
    dot_general x1, matrix products, on_device(): jnp.dot(normalized_rows, combined_probe_matrix, preferred_element_type=jn...  20.1 us
    all_to_all x1, blocking collectives, on_device(): lax.all_to_all(left_flat, 'res', split_axis=1, concat_axis=0, tiled=True)  18.1 us
  transfers between devices with their start and end apart: 5, of which 2 were waited for; matrix products, arithmetic and copies ran while one was open for 14% of the time, Pallas kernels for 0%

commit v1 on v0

v1 whole, which is shorter than its diff:
```python
import functools
import math

import jax
import jax.numpy as jnp
from jax import lax
from jax.experimental import pallas as pl
from jax.experimental.pallas import tpu as pltpu
from jax.sharding import PartitionSpec as P

LOG2E = math.log2(math.e)
VMEM_LIMIT = 60 * 1024 * 1024
CHUNKS = 4


def layer_normalize(inputs, scale_gain):
    sample_expectation = jnp.mean(inputs, axis=-1, keepdims=True)
    centered = inputs - sample_expectation
    variance = jnp.mean(centered * centered, axis=-1, keepdims=True)
    return centered * lax.rsqrt(variance + 1e-05) * scale_gain


def dot_f32(a, b, ca, cb):
    return lax.dot_general(a, b, (((ca,), (cb,)), ((), ())), preferred_element_type=jnp.float32)


def sequence_kernel(
    heads,
    pack,
    x_ref,
    bias_ref,
    gain_ref,
    probe_ref,
    offset_ref,
    final_ref,
    ff_gain_ref,
    widen_ref,
    shrink_ref,
    opm_gain_ref,
    left_w_ref,
    right_w_ref,
    out_ref,
    left_ref,
    right_ref,
    left_acc,
    right_acc,
):
    step = pl.program_id(0)
    steps = right_ref.shape[1]
    blocks, _, rows, width = x_ref.shape
    length = blocks * rows
    depth = width // heads
    x = x_ref[:, 0].astype(jnp.float32).reshape(length, width)
    normed = layer_normalize(x, gain_ref[...]).astype(jnp.bfloat16)
    mapped = dot_f32(probe_ref[...], normed, 1, 1)
    q = (mapped[:width] * (depth ** (-0.5) * LOG2E)).astype(jnp.bfloat16)
    k = mapped[width : 2 * width].astype(jnp.bfloat16)
    v = mapped[2 * width : 3 * width].astype(jnp.bfloat16)
    gate = jax.nn.sigmoid(mapped[3 * width :] + offset_ref[...])
    ones = jnp.ones((16, length), jnp.bfloat16)
    gated = []
    for h in range(heads):
        part = slice(h * depth, (h + 1) * depth)
        scores = dot_f32(k[part], q[part], 0, 0) + bias_ref[h]
        top = jnp.max(scores, axis=0, keepdims=True)
        p = jnp.exp2(scores - top).astype(jnp.bfloat16)
        mixed = dot_f32(jnp.concatenate([v[part], ones], axis=0), p, 1, 0)
        share = mixed[:depth] / mixed[depth : depth + 1]
        gated.append((share * gate[part]).astype(jnp.bfloat16))
    gated = jnp.concatenate(gated, axis=0)
    stream = x + dot_f32(gated, final_ref[...], 0, 0)
    normed = layer_normalize(stream, ff_gain_ref[...]).astype(jnp.bfloat16)
    hidden = jnp.maximum(dot_f32(normed, widen_ref[...], 1, 0), 0.0).astype(jnp.bfloat16)
    stream = stream + dot_f32(hidden, shrink_ref[...], 1, 0)
    updated = stream.astype(jnp.bfloat16)
    out_ref[:, 0] = stream.reshape(blocks, rows, width).astype(jnp.bfloat16)
    normed = layer_normalize(updated.astype(jnp.float32), opm_gain_ref[...]).astype(jnp.bfloat16)
    slot = lax.rem(step, pack)
    left = dot_f32(normed, left_w_ref[slot], 1, 0)

    @pl.when(slot == 0)
    def _():
        left_acc[...] = left

    @pl.when(slot != 0)
    def _():
        left_acc[...] = left_acc[...] + left

    left_ref[:, 0] = left_acc[...].reshape(blocks, rows, left.shape[1]).astype(jnp.bfloat16)
    factor = right_w_ref.shape[0]
    right = dot_f32(right_w_ref[...], normed, 1, 1)
    for e in range(factor):
        right_acc[e, pl.ds(step, 1), :] = right[e : e + 1]

    @pl.when(step == steps - 1)
    def _():
        right_ref[...] = right_acc[...].astype(jnp.bfloat16)


def run_sequences(x, bias, weights, heads, pack):
    blocks, steps, rows, width = x.shape
    length = blocks * rows
    factor = weights[-1].shape[0]
    whole = lambda a: pl.BlockSpec(
        a.shape, lambda s, n=a.ndim: (0,) * n, pipeline_mode=pl.Buffered(1)
    )
    lanes = pack * factor
    hidden = weights[5].shape[1]
    flops = 2 * length * width * (5 * width + 2 * hidden + 128) + 4 * length * length * width
    return pl.pallas_call(
        functools.partial(sequence_kernel, heads, pack),
        grid=(steps,),
        in_specs=[pl.BlockSpec((blocks, 1, rows, width), lambda s: (0, s, 0, 0)), whole(bias)]
        + [whole(a) for a in weights],
        out_specs=[
            pl.BlockSpec((blocks, 1, rows, width), lambda s: (0, s, 0, 0)),
            pl.BlockSpec((blocks, 1, rows, lanes), lambda s: (0, s // pack, 0, 0)),
            pl.BlockSpec((factor, steps, length), lambda s: (0, 0, 0)),
        ],
        out_shape=[
            jax.ShapeDtypeStruct(x.shape, jnp.bfloat16),
            jax.ShapeDtypeStruct((blocks, steps // pack, rows, lanes), jnp.bfloat16),
            jax.ShapeDtypeStruct((factor, steps, length), jnp.bfloat16),
        ],
        scratch_shapes=[
            pltpu.VMEM((length, lanes), jnp.float32),
            pltpu.VMEM((factor, steps, length), jnp.float32),
        ],
        compiler_params=pltpu.CompilerParams(
            dimension_semantics=("arbitrary",), vmem_limit_bytes=VMEM_LIMIT
        ),
        cost_estimate=pl.CostEstimate(
            flops=steps * flops * 3,
            bytes_accessed=bias.size * 4 + 4 * x.size,
            transcendentals=steps * heads * length * length,
        ),
        name="sequences",
    )(x, bias, *weights)


def product_kernel(rows, seq_total, left_ref, right_ref, table_ref, pair_ref, out_ref, stack):
    groups, factor, part, cols = right_ref.shape
    scale = 1.0 / seq_total
    left = left_ref[...]
    for e in range(factor):
        right = right_ref[:, e].reshape(groups * part, cols)
        outer = (dot_f32(left, right, 1, 0) * scale).astype(jnp.bfloat16)
        stack[:, e * factor : (e + 1) * factor, :] = outer.reshape(rows, factor, cols)
    for i in range(rows):
        update = dot_f32(table_ref[...], stack[i], 1, 0)
        out_ref[i] = (pair_ref[i].astype(jnp.float32) + update.T).astype(jnp.bfloat16)


def run_product(left, right, table, pair):
    total_rows, seq_total = left.shape
    groups, factor, part, cols = right.shape
    pair_rows = pair.shape[0]
    rows = math.gcd(pair_rows, 8)
    width = pair.shape[2]
    return pl.pallas_call(
        functools.partial(product_kernel, rows, seq_total),
        grid=(pair_rows // rows,),
        in_specs=[
            pl.BlockSpec((rows * factor, seq_total), lambda b: (b, 0)),
            pl.BlockSpec(right.shape, lambda b: (0, 0, 0, 0), pipeline_mode=pl.Buffered(1)),
            pl.BlockSpec(table.shape, lambda b: (0, 0), pipeline_mode=pl.Buffered(1)),
            pl.BlockSpec((rows, cols, width), lambda b: (b, 0, 0)),
        ],
        out_specs=pl.BlockSpec((rows, cols, width), lambda b: (b, 0, 0)),
        out_shape=jax.ShapeDtypeStruct(pair.shape, jnp.bfloat16),
        scratch_shapes=[pltpu.VMEM((rows, factor * factor, cols), jnp.bfloat16)],
        compiler_params=pltpu.CompilerParams(
            dimension_semantics=("arbitrary",), vmem_limit_bytes=VMEM_LIMIT
        ),
        cost_estimate=pl.CostEstimate(
            flops=4 * total_rows * cols * factor * (seq_total + width),
            bytes_accessed=2 * (right.size + left.size + 2 * pair.size),
            transcendentals=0,
        ),
        name="product",
    )(left, right, table, pair)


def on_device(
    aligned_activity,
    pair_state,
    focus_scaling_vector,
    combined_probe_matrix,
    sigmoid_offset_vector,
    focus_final_matrix,
    pair_norm_gain,
    pair_bias_matrix,
    feedforward_scaling_vector,
    feedforward_widen_matrix,
    feedforward_shrink_matrix,
    tensor_scaling_vector,
    twin_operand_matrix,
    tensor_final_matrix,
):
    width = aligned_activity.shape[2]
    heads = pair_bias_matrix.shape[1]
    factor = twin_operand_matrix.shape[1] // 2
    res_axis = lax.axis_size("res")
    seq_axis = lax.axis_size("seq")
    rows = aligned_activity.shape[1]
    seq_count = aligned_activity.shape[0] // res_axis
    length = rows * res_axis
    col_block = pair_state.shape[1]
    chunks = math.gcd(CHUNKS, seq_count)
    per_chunk = seq_count // chunks
    pack = math.gcd(per_chunk, 128 // factor)

    pieces = aligned_activity.reshape(res_axis, seq_count, rows, width)
    arrived = [
        lax.all_to_all(
            pieces[:, c * per_chunk : (c + 1) * per_chunk], "res", split_axis=0, concat_axis=0, tiled=True
        )
        for c in range(chunks)
    ]

    pair_norm = layer_normalize(pair_state.astype(jnp.float32), pair_norm_gain)
    bias_tile = jnp.einsum(
        "ijc,ch->hij", pair_norm, pair_bias_matrix, precision=lax.Precision.HIGHEST
    ).astype(jnp.bfloat16)
    bias_cols = lax.all_gather(bias_tile, "seq", axis=2, tiled=True)
    bias_all = lax.all_gather(bias_cols, "res", axis=1, tiled=True)
    bias = bias_all.transpose(0, 2, 1).astype(jnp.float32) * LOG2E

    left_w = twin_operand_matrix[:, :factor]
    left_w = jnp.stack(
        [jnp.pad(left_w, ((0, 0), (t * factor, (pack - 1 - t) * factor))) for t in range(pack)]
    )
    weights = (
        focus_scaling_vector.reshape(1, -1),
        combined_probe_matrix.T,
        sigmoid_offset_vector.reshape(-1, 1),
        focus_final_matrix,
        feedforward_scaling_vector.reshape(1, -1),
        feedforward_widen_matrix,
        feedforward_shrink_matrix,
        tensor_scaling_vector.reshape(1, -1),
        left_w,
        twin_operand_matrix[:, factor:].T,
    )
    returned, lefts, rights = [], [], []
    for c in range(chunks):
        updated, left, right = run_sequences(arrived[c], bias, weights, heads, pack)
        returned.append(
            lax.all_to_all(updated, "res", split_axis=0, concat_axis=0, tiled=True)
        )
        lefts.append(left)
        rights.append(right)
    alignment_output = jnp.concatenate(returned, axis=1).reshape(aligned_activity.shape)

    left = lax.all_to_all(
        jnp.concatenate(lefts, axis=1), "res", split_axis=0, concat_axis=0, tiled=True
    )
    left = lax.all_gather(left, "seq", axis=0)
    left = left.reshape(seq_axis, res_axis, seq_count // pack, rows, pack, factor)
    left = left.transpose(3, 5, 1, 0, 2, 4).reshape(rows * factor, -1)

    right = jnp.concatenate(rights, axis=1).reshape(factor, seq_count, seq_axis, col_block)
    right = right.transpose(2, 0, 1, 3)
    right = lax.all_to_all(right, "seq", split_axis=0, concat_axis=0, tiled=True)
    right = lax.all_gather(right, "res", axis=0, tiled=True)
    if seq_count % 16 != 0:
        right = right.transpose(1, 0, 2, 3).reshape(1, factor, -1, col_block)
        right = right.reshape(1, factor, -1, col_block)
    table = tensor_final_matrix.reshape(factor, factor, -1).transpose(2, 1, 0)
    table = table.reshape(table.shape[0], -1)
    pair_output = run_product(left, right, table, pair_state)
    return (alignment_output, pair_output)


def solution(mesh):
    return jax.shard_map(
        on_device,
        mesh=mesh,
        in_specs=(
            P(("grp", "seq"), "res", None),
            P(("grp", "res"), "seq", None),
            P(),
            P(),
            P(),
            P(),
            P(),
            P(),
            P(),
            P(),
            P(),
            P(),
            P(),
            P(),
        ),
        out_specs=(P(("grp", "seq"), "res", None), P(("grp", "res"), "seq", None)),
        check_vma=False,
    )
```

time: 856 us -> 523 us (0.61)
  matrix products: 270 us -> 12.9 us
  local copies, waits for them, and re-layouts: 230 us -> 29.9 us
  Pallas kernels: 0 us -> 142 us
  blocking collectives: 25.3 us -> 162 us
  waiting for transfers between devices: 250 us -> 118 us
  other arithmetic: 40.2 us -> 21.3 us
  starting transfers between devices: 12.1 us -> 21.4 us
    all_to_all x2 -> x5, waiting for transfers between devices: 250 us -> 62.5 us  [the longest x2 62.5 us: on_device(): lax.all_to_all(updated, 'res', split_axis=0, concat_axis=0, tiled=True)]
    dot_general x14 -> x0, matrix products: 169 us -> none  [the longest x8 65.9 us: one_block(): jnp.einsum('shnj,sjhd->snhd', softmax_shares, content_entries, preferred_...]
    pallas_call x0 -> x5, Pallas kernels: none -> 142 us  [the longest x4 124 us: run_sequences(): pl.pallas_call(functools.partial(sequence_kernel, heads, pack), grid=(ste...]
    all_to_all x2 -> x5, blocking collectives: 23 us -> 160 us  [the longest x2 85.6 us: on_device(): lax.all_to_all(updated, 'res', split_axis=0, concat_axis=0, tiled=True)]
    reshape x2 -> x5, local copies, waits for them, and re-layouts: 128 us -> 9.08 us  [the longest x2 7.32 us: on_device(): left = left.transpose(3, 5, 1, 0, 2, 4).reshape(rows * factor, -1)]
    sub x8 -> x0, matrix products: 88.2 us -> none  [one_block(): exponent = jnp.exp(scores - top_score)]
    all_gather x1, waiting for transfers between devices: 0.01 us -> 54.4 us  [on_device(): bias_all = lax.all_gather(bias_cols, 'res', axis=1, tiled=True)]
    convert_element_type x4 -> x0, local copies, waits for them, and re-layouts: 27.5 us -> none  [the longest x2 13.2 us: on_device(): residual_state = input_rows.astype(jnp.float32)]
  transfers between devices with their start and end apart: 5 -> 8, of which waited for: 2 -> 3; matrix products, arithmetic and copies ran while one was open for 14% -> 8% of each run, Pallas kernels for 0% -> 18%
where the time goes in v1:
time: 523 us; the launch traced here: 522 us
  blocking collectives  162 us (31%)
  Pallas kernels  142 us (27%)
  waiting for transfers between devices  118 us (23%)
  local copies, waits for them, and re-layouts  29.9 us (6%)
  starting transfers between devices  21.4 us (4%)
  other arithmetic  21.3 us (4%)
  between operations  14.1 us (3%)
  matrix products  12.9 us (2%)
    pallas_call x4, Pallas kernels, run_sequences(): pl.pallas_call(functools.partial(sequence_kernel, heads, pack), grid=(ste...  124 us
    all_to_all x2, blocking collectives, on_device(): lax.all_to_all(updated, 'res', split_axis=0, concat_axis=0, tiled=True)  85.6 us
    all_to_all x2, waiting for transfers between devices, on_device(): lax.all_to_all(updated, 'res', split_axis=0, concat_axis=0, tiled=True)  62.5 us
    all_gather x1, waiting for transfers between devices, on_device(): bias_all = lax.all_gather(bias_cols, 'res', axis=1, tiled=True)  54.4 us
    all_to_all x1, blocking collectives, on_device(): lax.all_to_all(pieces[:, c * per_chunk:(c + 1) * per_chunk], 'res', split...  50.1 us
    all_to_all x1, blocking collectives, on_device(): lax.all_to_all(jnp.concatenate(lefts, axis=1), 'res', split_axis=0, conca...  19.3 us
    pallas_call x1, Pallas kernels, run_product(): pl.pallas_call(functools.partial(product_kernel, rows, seq_total), grid=(...  18.8 us
    all_to_all x3, starting transfers between devices, on_device(): lax.all_to_all(pieces[:, c * per_chunk:(c + 1) * per_chunk], 'res', split...  13.2 us
  transfers between devices with their start and end apart: 8, of which 3 were waited for; matrix products, arithmetic and copies ran while one was open for 8% of the time, Pallas kernels for 18%

profile of v1, /device:TPU:0, one launch (start us, length us, event | category | flops | bytes accessed | tf_op | source)
XLA Modules:
  0.0 521.8 jit_solution(10884560756641808642)
XLA Ops:
  7.2 0.0 copy-start
  7.2 0.0 all-gather.5.cloned.1.call-start
  7.2 0.0 copy-start.2
  7.2 3.5 convert_reduce_fusion
  10.8 4.8 fusion.2
  15.6 0.0 copy-done
  15.6 0.0 copy-done.16
  15.6 12.9 %fusion.12 = bf16[8,64,256]{2,0,1:T(8,128)(2,1)S(1)} fusion(bf16[64,256,128]{2,1,0:T(8,128)(2,1)S(1)} %copy-done.2, f32[128]{0:T(128)S(1)} %copy-done.16, f32[64,256]{1,0:T(8,128)S(1)} %add_rsqrt_fusion, f32[64,256]{1,0:T(8,128)S(1)} %broadcast_multiply_fusion, f32[128,8]{0,1:T(8,128)S(1)} %copy-done), kind=kOutput, calls=%fused_computation.13 | convolution fusion | flops 209846272 | bytes 4592128 | tf_op jit(solution)/shard_map/ijc,ch->hij/dot_general | solution.py:222
  28.5 2.4 all_gather.15
  30.9 0.0 all-gather.5.cloned.1.call-update
  30.9 4.1 fusion.16
  35.0 50.1 %all_to_all.50.x_ref = bf16[8,4,64,256]{3,2,1,0:T(8,128)(2,1)} all-to-all(bf16[8,4,64,256]{3,2,1,0:T(8,128)(2,1)S(1)} %get-tuple-element.26), channel_id=1, replica_groups=mesh['grp'=2,'res'=8,'seq'=2] {'res'}, dimensions={0} | all-to-all | bytes 2097152 | tf_op jit(solution)/shard_map/all_to_all | solution.py:215
  85.1 3.6 all-to-all-start.2
  88.7 0.6 slice_bitcast_fusion
  89.3 0.1 copy.72
  89.4 1.0 copy.60
  90.5 0.0 copy-done.15
  90.5 0.8 copy.62.offset_ref
  91.3 0.1 pad_bitcast_fusion.3
  91.4 0.7 pad_maximum_fusion.3.left_w_ref
  92.1 54.4 %all-gather.5.cloned.1.call-done = bf16[8,512,512]{2,0,1:T(8,128)(2,1)} async-done(((bf16[8,64,512]{2,0,1:T(8,128)(2,1)}), bf16[8,512,512]{2,0,1:T(8,128)(2,1)}) %all-gather.5.cloned.1.call-update) | async-done | bytes 4194320 | tf_op jit(solution)/shard_map/all_gather | solution.py:226
  146.5 7.5 %copy.59 = bf16[8,512,512]{1,2,0:T(8,128)(2,1)} copy(bf16[8,512,512]{2,0,1:T(8,128)(2,1)} %all-gather.5.cloned.1.call-done) | data formatting | bytes 8388608 | tf_op jit(solution)/shard_map/all_gather | solution.py:226
  154.0 0.0 all-to-all-done.2.x_ref
  154.0 3.6 all-to-all-start.4
  157.6 6.7 %multiply_bitcast_fusion.bias_ref = f32[8,512,512]{2,1,0:T(8,128)} fusion(bf16[8,512,512]{1,2,0:T(8,128)(2,1)} %copy.59), kind=kLoop, calls=%fused_computation.7 | loop fusion | flops 4194304 | bytes 12582912 | tf_op jit(solution)/shard_map/mul | solution.py:227
  164.3 30.9 %sequences.4 = (bf16[8,4,64,256]{3,2,1,0:T(8,128)(2,1)}, bf16[8,1,64,128]{3,2,1,0:T(8,128)(2,1)}, bf16[32,4,512]{2,1,0:T(4,128)(2,1)}) custom-call(bf16[8,4,64,256]{3,2,1,0:T(8,128)(2,1)} %all_to_all.50.x_ref, f32[8,512,512]{2,1,0:T(8,128)} %multiply_bitcast_fusion.bias_ref, f32[1,256]{1,0:T(1,128)} %bitcast.47, bf16[1024,256]{1,0:T(8,128)(2,1)} %bitcast.41, ...), custom_call_target="tpu_custom_call" | custom-call | flops 14092861440 | bytes 10485760 | tf_op jit(solution)/shard_map/sequences/pallas_call | solution.py:110
  195.2 0.0 all-to-all-done.4.x_ref
  195.2 0.0 copy-start.5
  195.2 6.0 %all-to-all-start.6 = ((bf16[8,4,64,256]{3,2,1,0:T(8,128)(2,1)}), bf16[8,4,64,256]{3,2,1,0:T(8,128)(2,1)S(1)}, u32[]{:S(2)}, u32[]{:S(2)}) async-start(bf16[8,4,64,256]{3,2,1,0:T(8,128)(2,1)} %get-tuple-element.27), calls=%async_computation.6 | async-start | bytes 2097152 | tf_op jit(solution)/shard_map/all_to_all | solution.py:215
  201.2 0.2 all-gather.9.cloned.1.call-start
  201.5 30.9 %sequences.5 = (bf16[8,4,64,256]{3,2,1,0:T(8,128)(2,1)}, bf16[8,1,64,128]{3,2,1,0:T(8,128)(2,1)}, bf16[32,4,512]{2,1,0:T(4,128)(2,1)}) custom-call(bf16[8,4,64,256]{3,2,1,0:T(8,128)(2,1)} %copy-done.4, f32[8,512,512]{2,1,0:T(8,128)} %multiply_bitcast_fusion.bias_ref, f32[1,256]{1,0:T(1,128)} %bitcast.48, bf16[1024,256]{1,0:T(8,128)(2,1)} %bitcast.42, ...), custom_call_target="tpu_custom_call" | custom-call | flops 14092861440 | bytes 10485760 | tf_op jit(solution)/shard_map/sequences/pallas_call | solution.py:110
  232.4 30.9 %sequences.6 = (bf16[8,4,64,256]{3,2,1,0:T(8,128)(2,1)}, bf16[8,1,64,128]{3,2,1,0:T(8,128)(2,1)}, bf16[32,4,512]{2,1,0:T(4,128)(2,1)}) custom-call(bf16[8,4,64,256]{3,2,1,0:T(8,128)(2,1)} %copy-done.5, f32[8,512,512]{2,1,0:T(8,128)} %multiply_bitcast_fusion.bias_ref, f32[1,256]{1,0:T(1,128)} %bitcast.49, bf16[1024,256]{1,0:T(8,128)(2,1)} %bitcast.43, ...), custom_call_target="tpu_custom_call" | custom-call | flops 14092861440 | bytes 10485760 | tf_op jit(solution)/shard_map/sequences/pallas_call | solution.py:110
  263.4 0.0 copy-start.9
  263.4 0.0 copy-start.12
  263.4 0.0 copy-start.13
  263.4 0.0 copy-start.8
  263.4 0.0 copy-start.10
  263.4 0.0 all-to-all-done.6.x_ref
  263.4 0.0 copy-start.6
  263.4 1.0 copy-done.6
  264.4 30.8 %sequences.7 = (bf16[8,4,64,256]{3,2,1,0:T(8,128)(2,1)}, bf16[8,1,64,128]{3,2,1,0:T(8,128)(2,1)}, bf16[32,4,512]{2,1,0:T(4,128)(2,1)}) custom-call(bf16[8,4,64,256]{3,2,1,0:T(8,128)(2,1)} %copy-done.6, f32[8,512,512]{2,1,0:T(8,128)} %multiply_bitcast_fusion.bias_ref, f32[1,256]{1,0:T(1,128)} %bitcast.50, bf16[1024,256]{1,0:T(8,128)(2,1)} %bitcast.44, ...), custom_call_target="tpu_custom_call" | custom-call | flops 14092861440 | bytes 10485760 | tf_op jit(solution)/shard_map/sequences/pallas_call | solution.py:110
  295.3 1.0 pad_maximum_fusion.1
  296.3 19.3 %all_to_all.51 = bf16[8,4,64,128]{3,2,1,0:T(8,128)(2,1)} all-to-all(bf16[8,4,64,128]{3,2,1,0:T(8,128)(2,1)S(1)} %pad_maximum_fusion.1), channel_id=1, replica_groups=mesh['grp'=2,'res'=8,'seq'=2] {'res'}, dimensions={0} | all-to-all | bytes 1048576 | tf_op jit(solution)/shard_map/all_to_all | solution.py:255
  315.6 0.0 all-gather.9.cloned.1.call-update
  315.6 1.3 pad_maximum_fusion.2
  316.9 0.1 reshape.58
  317.1 0.1 copy.68
  317.1 4.9 all_to_all.52
  322.0 3.6 all-to-all-start.1
  325.7 0.0 all-gather.7.cloned.1.call-start
  325.7 0.7 all-gather.7.cloned.1.call-update
  326.4 38.7 %all-to-all-done.1 = bf16[8,4,64,256]{3,2,1,0:T(8,128)(2,1)S(1)} async-done(((bf16[8,4,64,256]{3,2,1,0:T(8,128)(2,1)}), bf16[8,4,64,256]{3,2,1,0:T(8,128)(2,1)S(1)}, u32[]{:S(2)}, u32[]{:S(2)}) %all-to-all-start.1) | async-done | bytes 1048608 | tf_op jit(solution)/shard_map/all_to_all | solution.py:249
  365.1 54.8 %all_to_all.53 = bf16[8,4,64,256]{3,2,1,0:T(8,128)(2,1)S(1)} all-to-all(bf16[8,4,64,256]{3,2,1,0:T(8,128)(2,1)S(1)} %copy-done.3), channel_id=1, replica_groups=mesh['grp'=2,'res'=8,'seq'=2] {'res'}, dimensions={0} | all-to-all | bytes 2097152 | tf_op jit(solution)/shard_map/all_to_all | solution.py:249
  419.9 30.8 %all_to_all.54 = bf16[8,4,64,256]{3,2,1,0:T(8,128)(2,1)S(1)} all-to-all(bf16[8,4,64,256]{3,2,1,0:T(8,128)(2,1)} %get-tuple-element.16), channel_id=1, replica_groups=mesh['grp'=2,'res'=8,'seq'=2] {'res'}, dimensions={0} | all-to-all | bytes 2097152 | tf_op jit(solution)/shard_map/all_to_all | solution.py:249
  450.7 4.3 all-to-all-start.7
  455.0 1.1 copy.69
  456.1 0.9 copy.71.table_ref
  456.9 23.7 %all-to-all-done.7 = bf16[8,4,64,256]{3,2,1,0:T(8,128)(2,1)} async-done(((bf16[8,4,64,256]{3,2,1,0:T(8,128)(2,1)}), bf16[8,4,64,256]{3,2,1,0:T(8,128)(2,1)}, u32[]{:S(2)}, u32[]{:S(2)}) %all-to-all-start.7) | async-done | bytes 1048608 | tf_op jit(solution)/shard_map/all_to_all | solution.py:249
  480.7 3.3 pad_maximum_fusion
  484.0 2.0 copy.66
  486.0 3.2 copy.67
  489.2 6.0 %reshape.57 = bf16[2048,256]{0,1:T(8,128)(2,1)S(1)} reshape(bf16[64,32,8,2,4,4]{1,0,5,4,3,2:T(8,128)(2,1)} %copy.67) | data formatting | bytes 2097152 | tf_op jit(solution)/shard_map/reshape | solution.py:260
  495.2 1.3 copy.70.left_ref
  496.5 18.8 %product.1 = bf16[64,256,128]{2,1,0:T(8,128)(2,1)} custom-call(bf16[2048,256]{1,0:T(8,128)(2,1)} %copy.70.left_ref, bf16[16,32,16,256]{3,2,1,0:T(8,128)(2,1)} %all-gather.7.cloned.1.call-done.right_ref, bf16[128,1024]{1,0:T(8,128)(2,1)} %copy.71.table_ref, bf16[64,256,128]{2,1,0:T(8,128)(2,1)} %pair_ref.1), custom_call_target="tpu_custom_call" | custom-call | flops 25769803776 | bytes 13631488 | tf_op jit(solution)/shard_map/product/pallas_call | solution.py:160
  (25 shorter events, 0.1 us)
Async XLA Ops:
  7.2 8.4 %copy-start = (f32[128,8]{0,1:T(8,128)S(1)}, f32[128,8]{0,1:T(8,128)}, u32[]{:S(2)}) copy-start(f32[128,8]{0,1:T(8,128)} %param.21) | copy-start | bytes 12292
  7.2 8.4 %copy-start.16 = (f32[128]{0:T(128)S(1)}, f32[128]{0:T(128)}, u32[]{:S(2)}) copy-start(f32[128]{0:T(128)} %param.20) | copy-start | bytes 1540
  7.2 139.3 %all-gather.5.cloned.1.call-start = ((), (), s32[]{:S(2)}) async-start(), calls=%async_computation.10 | async-start | bytes 4718592 | tf_op jit(solution)/shard_map/all_gather | solution.py:226
  7.2 3.5 copy-start.2
  35.0 53.7 %copy-start.14 = (bf16[256,64]{0,1:T(8,128)(2,1)S(1)}, bf16[256,64]{0,1:T(8,128)(2,1)}, u32[]{:S(2)}) copy-start(bf16[256,64]{0,1:T(8,128)(2,1)} %param.26) | copy-start | bytes 98308
  35.0 54.4 %copy-start.7 = (bf16[256,1024]{1,0:T(8,128)(2,1)S(1)}, bf16[256,1024]{1,0:T(8,128)(2,1)}, u32[]{:S(2)}) copy-start(bf16[256,1024]{1,0:T(8,128)(2,1)} %param.17) | copy-start | bytes 1572868
  35.0 55.4 %copy-start.15 = (f32[256]{0:T(256)S(1)}, f32[256]{0:T(256)}, u32[]{:S(2)}) copy-start(f32[256]{0:T(256)} %param.18) | copy-start | bytes 3076
  85.1 68.9 %all-to-all-start.2 = ((bf16[8,4,64,256]{3,2,1,0:T(8,128)(2,1)}), bf16[8,4,64,256]{3,2,1,0:T(8,128)(2,1)S(1)}, u32[]{:S(2)}, u32[]{:S(2)}) async-start(bf16[8,4,64,256]{3,2,1,0:T(8,128)(2,1)} %get-tuple-element.29), calls=%async_computation.2 | async-start | bytes 2097152 | tf_op jit(solution)/shard_map/all_to_all | solution.py:215
  154.0 10.3 %copy-start.4 = (bf16[8,4,64,256]{3,2,1,0:T(8,128)(2,1)}, bf16[8,4,64,256]{3,2,1,0:T(8,128)(2,1)S(1)}, u32[]{:S(2)}) copy-start(bf16[8,4,64,256]{3,2,1,0:T(8,128)(2,1)S(1)} %all-to-all-done.2.x_ref) | copy-start | bytes 3145732
  154.0 41.2 %all-to-all-start.4 = ((bf16[8,4,64,256]{3,2,1,0:T(8,128)(2,1)}), bf16[8,4,64,256]{3,2,1,0:T(8,128)(2,1)S(1)}, u32[]{:S(2)}, u32[]{:S(2)}) async-start(bf16[8,4,64,256]{3,2,1,0:T(8,128)(2,1)} %get-tuple-element.28), calls=%async_computation.4 | async-start | bytes 2097152 | tf_op jit(solution)/shard_map/all_to_all | solution.py:215
  195.2 37.2 %copy-start.5 = (bf16[8,4,64,256]{3,2,1,0:T(8,128)(2,1)}, bf16[8,4,64,256]{3,2,1,0:T(8,128)(2,1)S(1)}, u32[]{:S(2)}) copy-start(bf16[8,4,64,256]{3,2,1,0:T(8,128)(2,1)S(1)} %all-to-all-done.4.x_ref) | copy-start | bytes 3145732
  195.2 68.2 %all-to-all-start.6 = ((bf16[8,4,64,256]{3,2,1,0:T(8,128)(2,1)}), bf16[8,4,64,256]{3,2,1,0:T(8,128)(2,1)S(1)}, u32[]{:S(2)}, u32[]{:S(2)}) async-start(bf16[8,4,64,256]{3,2,1,0:T(8,128)(2,1)} %get-tuple-element.27), calls=%async_computation.6 | async-start | bytes 2097152 | tf_op jit(solution)/shard_map/all_to_all | solution.py:215
  201.2 282.7 %all-gather.9.cloned.1.call-start = ((), (), s32[]{:S(2)}) async-start(), calls=%async_computation.12 | async-start | bytes 1572864 | tf_op jit(solution)/shard_map/all_gather | solution.py:258
  263.4 31.9 %copy-start.9 = (bf16[8,1,64,128]{3,2,1,0:T(8,128)(2,1)S(1)}, bf16[8,1,64,128]{3,2,1,0:T(8,128)(2,1)}, u32[]{:S(2)}) copy-start(bf16[8,1,64,128]{3,2,1,0:T(8,128)(2,1)} %get-tuple-element.18) | copy-start | bytes 393220
  263.4 31.9 %copy-start.12 = (bf16[8,1,64,128]{3,2,1,0:T(8,128)(2,1)S(1)}, bf16[8,1,64,128]{3,2,1,0:T(8,128)(2,1)}, u32[]{:S(2)}) copy-start(bf16[8,1,64,128]{3,2,1,0:T(8,128)(2,1)} %get-tuple-element.19) | copy-start | bytes 393220
  263.4 31.9 %copy-start.13 = (bf16[8,1,64,128]{3,2,1,0:T(8,128)(2,1)S(1)}, bf16[8,1,64,128]{3,2,1,0:T(8,128)(2,1)}, u32[]{:S(2)}) copy-start(bf16[8,1,64,128]{3,2,1,0:T(8,128)(2,1)} %get-tuple-element.20) | copy-start | bytes 393220
  263.4 52.2 %copy-start.8 = (bf16[32,4,512]{2,1,0:T(4,128)(2,1)S(1)}, bf16[32,4,512]{2,1,0:T(4,128)(2,1)}, u32[]{:S(2)}) copy-start(bf16[32,4,512]{2,1,0:T(4,128)(2,1)} %get-tuple-element.22) | copy-start | bytes 393220
  263.4 52.2 %copy-start.10 = (bf16[32,4,512]{2,1,0:T(4,128)(2,1)S(1)}, bf16[32,4,512]{2,1,0:T(4,128)(2,1)}, u32[]{:S(2)}) copy-start(bf16[32,4,512]{2,1,0:T(4,128)(2,1)} %get-tuple-element.23) | copy-start | bytes 393220
  263.4 52.2 %copy-start.11 = (bf16[32,4,512]{2,1,0:T(4,128)(2,1)S(1)}, bf16[32,4,512]{2,1,0:T(4,128)(2,1)}, u32[]{:S(2)}) copy-start(bf16[32,4,512]{2,1,0:T(4,128)(2,1)} %get-tuple-element.24) | copy-start | bytes 393220
  263.4 1.0 copy-start.6
  296.2 68.9 %copy-start.3 = (bf16[8,4,64,256]{3,2,1,0:T(8,128)(2,1)S(1)}, bf16[8,4,64,256]{3,2,1,0:T(8,128)(2,1)}, u32[]{:S(2)}) copy-start(bf16[8,4,64,256]{3,2,1,0:T(8,128)(2,1)} %get-tuple-element.15) | copy-start | bytes 3145732
  322.0 43.1 %all-to-all-start.1 = ((bf16[8,4,64,256]{3,2,1,0:T(8,128)(2,1)}), bf16[8,4,64,256]{3,2,1,0:T(8,128)(2,1)S(1)}, u32[]{:S(2)}, u32[]{:S(2)}) async-start(bf16[8,4,64,256]{3,2,1,0:T(8,128)(2,1)} %get-tuple-element.14), calls=%async_computation.1 | async-start | bytes 2097152 | tf_op jit(solution)/shard_map/all_to_all | solution.py:249
  325.7 170.8 %all-gather.7.cloned.1.call-start = ((), (), s32[]{:S(2)}) async-start(), calls=%async_computation.11 | async-start | bytes 4718592 | tf_op jit(solution)/shard_map/all_gather | solution.py:265
  450.7 29.9 %all-to-all-start.7 = ((bf16[8,4,64,256]{3,2,1,0:T(8,128)(2,1)}), bf16[8,4,64,256]{3,2,1,0:T(8,128)(2,1)}, u32[]{:S(2)}, u32[]{:S(2)}) async-start(bf16[8,4,64,256]{3,2,1,0:T(8,128)(2,1)} %get-tuple-element.17), calls=%async_computation.7 | async-start | bytes 2097152 | tf_op jit(solution)/shard_map/all_to_all | solution.py:249
  496.5 18.8 %copy-start.1 = (f32[128,8]{0,1:T(8,128)S(1)}, f32[128,8]{0,1:T(8,128)}, u32[]{:S(2)}) copy-start(f32[128,8]{0,1:T(8,128)} %param.21) | copy-start | bytes 12292
Sparse Core Ops, SparseCore 0:
  31.1 115.4 all-gather.4
  315.7 8.0 all-gather.8
  328.6 114.6 all-gather.6
